TPU v7x, 512 devices: a whole 4x8x8 slice. The times are simulated.
512 devices in a mesh: section: 16 (over z_lo, y), seq: 32 (over x, z_hi, core).
Axes of the slice: x: 4, y: 8, z: 8 (z_hi: 4, z_lo: 2; z = z_hi * 2 + z_lo), core: 2. Of those that a mesh axis runs over, the one named last changes fastest.
Arguments:
- hidden: bfloat16 [16, 4096, 2048], P('section', 'seq'), may hold values from -6 to 6
- query_gain: bfloat16 [16, 2048], P('section'), may hold values from 0.099609375 to 1.8984375
- out_gain: bfloat16 [16, 2048], P('section'), may hold values from 0.099609375 to 1.8984375
- keys_now: bfloat16 [16, 4096, 512], P('section', 'seq'), may hold values from -26.516504 to 26.516504
- values_now: bfloat16 [16, 4096, 512], P('section', 'seq'), may hold values from -6 to 6
- keys_cached: bfloat16 [16, 4096, 512], P('section', 'seq'), may hold values from -6 to 6
- values_cached: bfloat16 [16, 4096, 512], P('section', 'seq'), may hold values from -6 to 6
- first_key: int32 [16], P('section'), may hold values from 0 to 4096
Outputs:
- handoff: bfloat16 [16, 4096, 2048], P('section', 'seq')
All inputs are finite; a program needn't handle non-finite values.
Results may differ from a plain program's by a relative error of at most 0.0065.
Values may be sent and summed in bfloat16 or wider, within the bound.
No kernel may reach another device: no remote copies, remote signals or barrier semaphores. Data moves between devices by JAX's collectives and lax.ppermute only.
A program may use at most 128 MiB of HBM per device.

v0:
```python
import functools
import math

import jax
import jax.numpy as jnp
from jax import lax
from jax.experimental import pallas as pl
from jax.experimental.pallas import tpu as pltpu
from jax.sharding import PartitionSpec as P


HEADS = 16
KV_HEADS = 4
HEAD = 128
GROUP = HEADS // KV_HEADS
BLK = 128
XS = 4
ZS = 4
SECTIONS = 16
SEQ = 32
MASKED = -1e30
EXP2_SCALE = HEAD**-0.5 * math.log2(math.e)
ROUNDS = (0, 1, 3, 2)
TILE = 256
BLOCKS = 33
GAIN_ROWS = 16 * KV_HEADS


def seq_of(x, z, c):
    return (x % XS) * 8 + (z % ZS) * 2 + c


def sign(c):
    return 1 - 2 * c


def along_z(r):
    return [(seq_of(x, z, c), seq_of(x, z + sign(c) * r, c)) for x in range(XS) for z in range(ZS) for c in range(2)]


def along_x(r):
    return [(seq_of(x, z, c), seq_of(x + sign(c) * r, z, c)) for x in range(XS) for z in range(ZS) for c in range(2)]


def home_pairs(r):
    return [
        (s * SEQ + seq_of(x, z, c), (s + 1) % SECTIONS * SEQ + seq_of(x, z - sign(c) * r, c))
        for s in range(SECTIONS)
        for x in range(XS)
        for z in range(ZS)
        for c in range(2)
    ]


Z_GROUPS = [[seq_of(x, z, c) for z in range(ZS)] for x in range(XS) for c in range(2)]
OTHER_CORE = [(q, q ^ 1) for q in range(SEQ)]


def nt(a, b):
    return lax.dot_general(a, b, (((1,), (1,)), ((), ())), preferred_element_type=jnp.float32)


def attention_kernel(meta, q_ref, own_ref, other_ref, far_ref, far_other_ref, gain_ref, o_ref, s_ref, *, kq):
    cols = lax.broadcasted_iota(jnp.int32, (BLK, BLK), 1)
    rows = lax.broadcasted_iota(jnp.int32, (BLK, BLK), 0)
    limit, me = meta[0], meta[1]
    x, z, c = me // 8, (me // 2) % 4, me % 2
    sg = 1 - 2 * c
    row_base = x * 8 * BLK
    place = [[2 * ((z - flip * r + 4) % 4) + core for r in ROUNDS] for flip, core in ((sg, c), (-sg, 1 - c))]
    diag = place[0][kq]
    heads = TILE // BLK
    q_at = z if kq == 0 else (z - sg * ROUNDS[kq] + 4) % 4
    blocks = []
    for half, ref in ((0, far_ref), (1, far_other_ref)):
        flip = -sg if half else sg
        for i in range(3):
            source = (x - flip * ROUNDS[i + 1] + 4) % 4
            for k in range(4):
                start = jnp.where(source > x, limit - BLK * (8 * source + place[half][k]), 0)
                blocks.append((ref, (i, k, 0), (i, k, 1), cols >= start))
    for half, ref in ((0, own_ref), (1, other_ref)):
        for k in range(4):
            if half == 0 and k == kq:
                continue
            at = place[half][k]
            cached = (at > diag).astype(jnp.int32) * 2
            start = jnp.where(at > diag, limit - (row_base + at * BLK), 0)
            blocks.append((ref, (k, cached), (k, cached + 1), cols >= start))
    blocks.append((own_ref, (kq, 0), (kq, 1), cols <= rows))
    blocks.append((own_ref, (kq, 2), (kq, 3), (cols > rows) & (cols >= limit - (row_base + diag * BLK))))
    pairs = [blocks[j : j + 2] for j in range(0, len(blocks), 2)]
    for t in range(GROUP // heads):
        lanes = [slice((t * heads + h) * BLK, (t * heads + h + 1) * BLK) for h in range(heads)]
        q = jnp.concatenate([q_ref[q_at, :, lane] for lane in lanes], 0)
        best = None
        for j, pair in enumerate(pairs):
            scores = nt(q, jnp.concatenate([ref[k_at] for ref, k_at, _, _ in pair], 0))
            for u, (_, _, _, mask) in enumerate(pair):
                part = jnp.where(jnp.concatenate([mask] * heads, 0), scores[:, u * BLK : (u + 1) * BLK], MASKED)
                s_ref[t % 2, :, (2 * j + u) * BLK : (2 * j + u + 1) * BLK] = part
                best = part if best is None else jnp.maximum(best, part)
        highest = jnp.max(best, axis=1, keepdims=True) * EXP2_SCALE
        total = None
        for j, pair in enumerate(pairs):
            span = s_ref[t % 2, :, 2 * j * BLK : (2 * j + len(pair)) * BLK]
            weights = jnp.exp2(span * EXP2_SCALE - highest)
            values = jnp.concatenate([ref[v_at] for ref, _, v_at, _ in pair], 0)
            values = jnp.concatenate([values, jnp.ones_like(values)], 1)
            part = jnp.dot(weights.astype(jnp.bfloat16), values, preferred_element_type=jnp.float32)
            total = part if total is None else total + part
        out = (total[:, :BLK] / total[:, BLK:]).astype(jnp.bfloat16)
        for h in range(heads):
            o_ref[:BLK, (t * heads + h) * BLK : (t * heads + h + 1) * BLK] = out[h * BLK : (h + 1) * BLK]
    if kq == 0:
        for g in range(KV_HEADS):
            rows_of = slice(BLK + 16 * g, BLK + 16 * (g + 1))
            part = gain_ref[:, g * GROUP * HEAD : (g + 1) * GROUP * HEAD].astype(jnp.float32)
            o_ref[rows_of, :] = jnp.broadcast_to(part, (16, GROUP * HEAD)).astype(jnp.bfloat16)


def attend(meta, q, own, other, far, far_other, kq, gain):
    vmem = pl.BlockSpec(memory_space=pltpu.VMEM)
    rows = BLK + GAIN_ROWS if kq == 0 else BLK
    return pl.pallas_call(
        functools.partial(attention_kernel, kq=kq),
        out_shape=jax.ShapeDtypeStruct((rows, GROUP * HEAD), jnp.bfloat16),
        in_specs=[pl.BlockSpec(memory_space=pltpu.SMEM)] + [vmem] * 6,
        out_specs=vmem,
        scratch_shapes=[pltpu.VMEM((2, TILE, BLOCKS * BLK), jnp.float32)],
        compiler_params=pltpu.CompilerParams(vmem_limit_bytes=24 * 2**20),
        cost_estimate=pl.CostEstimate(flops=4 * 512 * 4096 * 128, bytes_accessed=2**20, transcendentals=0),
        name="attend",
    )(meta, q, own, other, far, far_other, gain)


def finish_kernel(meta, o0, o1, o2, o3, hidden_ref, out_ref):
    parts = [o[:BLK].astype(jnp.float32) for o in (o0, o1, o2, o3)]
    squares = None
    for part in parts:
        part = part * part
        part = part[:, :128] + part[:, 128:256] + part[:, 256:384] + part[:, 384:]
        squares = part if squares is None else squares + part
    scale = lax.rsqrt(jnp.sum(squares, axis=1, keepdims=True) / (HEADS * HEAD) + 1e-06)
    z, c = (meta[1] // 2) % 4, meta[1] % 2
    for r, part in zip(ROUNDS, parts):
        group = (z + (1 - 2 * c) * r + 4) % 4
        at = pl.ds(pl.multiple_of(group * 512, 512), 512)
        gain = o0[pl.ds(pl.multiple_of(BLK + 16 * group, 16), 16), :].astype(jnp.float32)[:1]
        out_ref[0, :, at] = (hidden_ref[0, :, at].astype(jnp.float32) + part * scale * gain).astype(jnp.bfloat16)


def finish(meta, parts, hidden_before):
    vmem = pl.BlockSpec(memory_space=pltpu.VMEM)
    return pl.pallas_call(
        finish_kernel,
        out_shape=jax.ShapeDtypeStruct((1, BLK, HEADS * HEAD), jnp.bfloat16),
        in_specs=[pl.BlockSpec(memory_space=pltpu.SMEM)] + [vmem] * 5,
        out_specs=vmem,
        compiler_params=pltpu.CompilerParams(vmem_limit_bytes=16 * 2**20),
        name="finish",
    )(meta, *parts, hidden_before)


def on_device(hidden, query_gain, out_gain, keys_now, values_now, keys_cached, values_cached, first_key):
    me = lax.axis_index("seq")
    x, z, c = me // 8, (me // 2) % 4, me % 2
    sg = 1 - 2 * c
    limit = first_key[0]

    def kv_of(head):
        return jnp.stack(
            [
                lax.dynamic_slice(a[0], (0, head * HEAD), (BLK, HEAD))
                for a in (keys_now, values_now, keys_cached, values_cached)
            ]
        )

    hidden_before = lax.ppermute(hidden, "section", [(s, (s + 1) % SECTIONS) for s in range(SECTIONS)])
    pieces = [kv_of(z)]
    for k, r in enumerate(ROUNDS[1:], 1):
        pieces.append(lax.ppermute(kv_of((z + sg * r) % 4), "seq", along_z(r)))
    own = jnp.stack(pieces)

    widened = hidden[0].astype(jnp.float32)
    scale = lax.rsqrt(jnp.mean(widened * widened, axis=-1, keepdims=True) + 1e-06)
    queries = (widened * scale * query_gain[0].astype(jnp.float32)).astype(jnp.bfloat16)
    by_group = jnp.transpose(queries.reshape(BLK, KV_HEADS, GROUP * HEAD), (1, 0, 2))
    gathered = lax.all_to_all(by_group, "seq", 0, 0, axis_index_groups=Z_GROUPS)

    far = []
    for k, r in enumerate(ROUNDS[1:], 1):
        target = (x + sg * r) % 4
        picked = lax.dynamic_slice_in_dim(own, jnp.where(target > x, 0, 2), 2, 1)
        far.append(lax.ppermute(picked, "seq", along_x(r)))
    other = lax.ppermute(own, "seq", OTHER_CORE)
    far = jnp.stack(far)
    far_other = lax.ppermute(far, "seq", OTHER_CORE)

    meta = jnp.stack([limit, me])
    parts = [None] * 4
    for k in (0, 3, 1, 2):
        attended = attend(meta, gathered if k else by_group, own, other, far, far_other, k, out_gain)
        parts[k] = lax.ppermute(attended, ("section", "seq"), home_pairs(ROUNDS[k]))
    return finish(meta, parts, hidden_before)


def solution(mesh):
    assert mesh.shape["section"] == SECTIONS and mesh.shape["seq"] == SEQ

    return jax.shard_map(
        on_device,
        mesh=mesh,
        in_specs=(
            P("section", "seq", None),
            P("section", None),
            P("section", None),
            P("section", "seq", None),
            P("section", "seq", None),
            P("section", "seq", None),
            P("section", "seq", None),
            P("section"),
        ),
        out_specs=P("section", "seq", None),
        check_vma=False,
    )
```

profile of v0, /device:TPU:112, one launch (start us, length us, event | category | flops | bytes accessed | tf_op | source)
XLA Modules:
  0.0 123.8 jit_solution(4268533905132832978)
XLA Ops:
  0.0 0.9 copy-done.4
  0.9 0.9 constant_dynamic-slice_fusion.15
  1.8 0.1 copy-done.5
  1.9 0.1 copy-done.6
  2.0 0.0 copy-start.3
  2.0 10.1 %collective-permute-start.2 = (bf16[4,128,128]{2,1,0:T(8,128)(2,1)S(1)}, bf16[4,128,128]{2,1,0:T(8,128)(2,1)S(1)}, u32[]{:S(2)}, u32[]{:S(2)}) collective-permute-start(bf16[4,128,128]{2,1,0:T(8,128)(2,1)S(1)} %pad_maximum_fusion.4), channel_id=1, source_target_pairs={{0,4},{1,5},{2,6},{3,7},{4,0},{5,1},{6,2},{7,3},{8,12},{9,13},{10,... | collective-permute-start | bytes 393224 | tf_op jit(solution)/shard_map/ppermute | solution.py:182
  12.2 1.9 %collective-permute-start.1 = (bf16[4,128,128]{2,1,0:T(8,128)(2,1)S(1)}, bf16[4,128,128]{2,1,0:T(8,128)(2,1)S(1)}, u32[]{:S(2)}, u32[]{:S(2)}) collective-permute-start(bf16[4,128,128]{2,1,0:T(8,128)(2,1)S(1)} %pad_maximum_fusion.3), channel_id=1, source_target_pairs={{0,6},{1,3},{2,0},{3,5},{4,2},{5,7},{6,4},{7,1},{8,14},{9,11},{10,... | collective-permute-start | bytes 393224 | tf_op jit(solution)/shard_map/ppermute | solution.py:182
  14.2 4.8 %collective-permute-start = (bf16[4,128,128]{2,1,0:T(8,128)(2,1)S(1)}, bf16[4,128,128]{2,1,0:T(8,128)(2,1)S(1)}, u32[]{:S(2)}, u32[]{:S(2)}) collective-permute-start(bf16[4,128,128]{2,1,0:T(8,128)(2,1)S(1)} %pad_maximum_fusion.2), channel_id=1, source_target_pairs={{0,2},{1,7},{2,4},{3,1},{4,6},{5,3},{6,0},{7,5},{8,10},{9,15},{10,... | collective-permute-start | bytes 393224 | tf_op jit(solution)/shard_map/ppermute | solution.py:182
  19.1 0.3 copy.9
  19.4 0.3 multiply_reduce_fusion
  19.7 0.0 collective-permute-done.2
  19.7 0.6 collective-permute-done.1
  20.3 4.3 %collective-permute-done = bf16[4,128,128]{2,1,0:T(8,128)(2,1)S(1)} collective-permute-done((bf16[4,128,128]{2,1,0:T(8,128)(2,1)S(1)}, bf16[4,128,128]{2,1,0:T(8,128)(2,1)S(1)}, u32[]{:S(2)}, u32[]{:S(2)}) %collective-permute-start) | collective-permute-done | bytes 131104 | tf_op jit(solution)/shard_map/ppermute | solution.py:182
  24.6 0.1 pad_maximum_fusion.1.own_ref
  24.6 0.0 copy-start.7
  24.6 0.1 constant_dynamic-slice_fusion.2
  24.7 4.9 %collective-permute-start.6 = (bf16[4,2,128,128]{3,2,1,0:T(8,128)(2,1)S(1)}, bf16[4,2,128,128]{3,2,1,0:T(8,128)(2,1)S(1)}, u32[]{:S(2)}, u32[]{:S(2)}) collective-permute-start(bf16[4,2,128,128]{3,2,1,0:T(8,128)(2,1)S(1)} %get-tuple-element.6), channel_id=1, source_target_pairs={{0,16},{1,17},{2,18},{3,19},{4,20},{5,21},{6,22},{7,23},{8,24},{9,... | collective-permute-start | bytes 786440 | tf_op jit(solution)/shard_map/ppermute | solution.py:195
  29.7 3.0 %collective-permute-start.5 = (bf16[4,2,128,128]{3,2,1,0:T(8,128)(2,1)S(1)}, bf16[4,2,128,128]{3,2,1,0:T(8,128)(2,1)S(1)}, u32[]{:S(2)}, u32[]{:S(2)}) collective-permute-start(bf16[4,2,128,128]{3,2,1,0:T(8,128)(2,1)S(1)} %get-tuple-element.7), channel_id=1, source_target_pairs={{0,24},{1,9},{2,26},{3,11},{4,28},{5,13},{6,30},{7,15},{8,0},{9,17... | collective-permute-start | bytes 786440 | tf_op jit(solution)/shard_map/ppermute | solution.py:195
  32.7 2.8 %collective-permute-start.4 = (bf16[4,2,128,128]{3,2,1,0:T(8,128)(2,1)S(1)}, bf16[4,2,128,128]{3,2,1,0:T(8,128)(2,1)}, u32[]{:S(2)}, u32[]{:S(2)}) collective-permute-start(bf16[4,2,128,128]{3,2,1,0:T(8,128)(2,1)S(1)} %get-tuple-element.5), channel_id=1, source_target_pairs={{0,8},{1,25},{2,10},{3,27},{4,12},{5,29},{6,14},{7,31},{8,16},{9,1... | collective-permute-start | bytes 786440 | tf_op jit(solution)/shard_map/ppermute | solution.py:195
  35.6 0.2 copy.10
  35.8 1.5 %collective-permute-done.6 = bf16[4,2,128,128]{3,2,1,0:T(8,128)(2,1)S(1)} collective-permute-done((bf16[4,2,128,128]{3,2,1,0:T(8,128)(2,1)S(1)}, bf16[4,2,128,128]{3,2,1,0:T(8,128)(2,1)S(1)}, u32[]{:S(2)}, u32[]{:S(2)}) %collective-permute-start.6) | collective-permute-done | bytes 262176 | tf_op jit(solution)/shard_map/ppermute | solution.py:195
  37.3 4.0 %collective-permute-done.5 = bf16[4,2,128,128]{3,2,1,0:T(8,128)(2,1)S(1)} collective-permute-done((bf16[4,2,128,128]{3,2,1,0:T(8,128)(2,1)S(1)}, bf16[4,2,128,128]{3,2,1,0:T(8,128)(2,1)S(1)}, u32[]{:S(2)}, u32[]{:S(2)}) %collective-permute-start.5) | collective-permute-done | bytes 262176 | tf_op jit(solution)/shard_map/ppermute | solution.py:195
  41.3 1.0 collective-permute-done.4
  42.3 1.0 pad_maximum_fusion.far_ref
  43.4 1.9 %collective-permute-start.7 = (bf16[3,4,2,128,128]{4,3,2,1,0:T(8,128)(2,1)S(1)}, bf16[3,4,2,128,128]{4,3,2,1,0:T(8,128)(2,1)S(1)}, u32[]{:S(2)}, u32[]{:S(2)}) collective-permute-start(bf16[3,4,2,128,128]{4,3,2,1,0:T(8,128)(2,1)S(1)} %pad_maximum_fusion.far_ref), channel_id=1, source_target_pairs={{0,1},{1,0},{2,3},{3,2},{4,5},{5,4},{6,7},{7,6},{8,9},{9,8},{10,11... | collective-permute-start | bytes 2359304 | tf_op jit(solution)/shard_map/ppermute | solution.py:198
  45.3 1.0 fusion.q_ref
  46.2 6.7 %all-to-all-start = ((bf16[4,128,512]{2,1,0:T(8,128)(2,1)}), bf16[4,128,512]{2,1,0:T(8,128)(2,1)S(1)}, u32[]{:S(2)}, u32[]{:S(2)}) async-start(bf16[4,128,512]{2,1,0:T(8,128)(2,1)} %fusion.q_ref), calls=%async_computation | async-start | bytes 1048576 | tf_op jit(solution)/shard_map/all_to_all | solution.py:189
  52.9 2.1 %collective-permute-start.3 = (bf16[4,4,128,128]{3,2,1,0:T(8,128)(2,1)S(1)}, bf16[4,4,128,128]{3,2,1,0:T(8,128)(2,1)S(1)}, u32[]{:S(2)}, u32[]{:S(2)}) collective-permute-start(bf16[4,4,128,128]{3,2,1,0:T(8,128)(2,1)S(1)} %pad_maximum_fusion.1.own_ref), channel_id=1, source_target_pairs={{0,1},{1,0},{2,3},{3,2},{4,5},{5,4},{6,7},{7,6},{8,9},{9,8},{10,11... | collective-permute-start | bytes 1572872 | tf_op jit(solution)/shard_map/ppermute | solution.py:196
  55.0 2.6 %collective-permute-start.12 = (bf16[1,128,2048]{2,1,0:T(8,128)(2,1)}, bf16[1,128,2048]{2,1,0:T(8,128)(2,1)S(1)}, u32[]{:S(2)}, u32[]{:S(2)}) collective-permute-start(bf16[1,128,2048]{2,1,0:T(8,128)(2,1)} %param.8), channel_id=1, source_target_pairs={{0,32},{32,64},{64,96},{96,128},{128,160},{160,192},{192,224},{224... | collective-permute-start | bytes 1572872 | tf_op jit(solution)/shard_map/ppermute | solution.py:179
  58.3 0.1 pad_add_fusion.meta
  58.3 0.0 collective-permute-done.3.other_ref
  58.3 0.0 collective-permute-done.7.far_other_ref
  58.4 5.3 %attend.4 = bf16[192,512]{1,0:T(8,128)(2,1)S(1)} custom-call(s32[2]{0:T(128)S(1)} %pad_add_fusion.meta, bf16[4,128,512]{2,1,0:T(8,128)(2,1)} %fusion.q_ref, bf16[4,4,128,128]{3,2,1,0:T(8,128)(2,1)S(1)} %pad_maximum_fusion.1.own_ref, bf16[4,4,128,128]{3,2,1,0:T(8,128)(2,1)S(1)} %collective-permute-done.3.other_ref, ...), custom_call_target="tpu_custom_call" | custom-call | flops 1073741824 | bytes 1048576 | tf_op jit(solution)/shard_map/attend/pallas_call | solution.py:125
  63.7 2.4 %collective-permute-start.8 = (bf16[192,512]{1,0:T(8,128)(2,1)S(1)}, bf16[192,512]{1,0:T(8,128)(2,1)S(1)}, u32[]{:S(2)}, u32[]{:S(2)}) collective-permute-start(bf16[192,512]{1,0:T(8,128)(2,1)S(1)} %attend.4), channel_id=1, source_target_pairs={{0,32},{1,33},{2,34},{3,35},{4,36},{5,37},{6,38},{7,39},{8,40},{9,... | collective-permute-start | bytes 589832 | tf_op jit(solution)/shard_map/ppermute | solution.py:204
  66.1 3.0 %all-to-all-done.q_ref = bf16[4,128,512]{2,1,0:T(8,128)(2,1)S(1)} async-done(((bf16[4,128,512]{2,1,0:T(8,128)(2,1)}), bf16[4,128,512]{2,1,0:T(8,128)(2,1)S(1)}, u32[]{:S(2)}, u32[]{:S(2)}) %all-to-all-start) | async-done | bytes 524320 | tf_op jit(solution)/shard_map/all_to_all | solution.py:189
  69.1 1.0 copy-done.1
  70.1 4.6 %attend.5 = bf16[128,512]{1,0:T(8,128)(2,1)S(1)} custom-call(s32[2]{0:T(128)S(1)} %pad_add_fusion.meta, bf16[4,128,512]{2,1,0:T(8,128)(2,1)S(1)} %all-to-all-done.q_ref, bf16[4,4,128,128]{3,2,1,0:T(8,128)(2,1)S(1)} %pad_maximum_fusion.1.own_ref, bf16[4,4,128,128]{3,2,1,0:T(8,128)(2,1)S(1)} %copy-done.1, ...), custom_call_target="tpu_custom_call" | custom-call | flops 1073741824 | bytes 1048576 | tf_op jit(solution)/shard_map/attend/pallas_call | solution.py:125
  74.7 4.8 %collective-permute-start.9 = (bf16[128,512]{1,0:T(8,128)(2,1)S(1)}, bf16[128,512]{1,0:T(8,128)(2,1)S(1)}, u32[]{:S(2)}, u32[]{:S(2)}) collective-permute-start(bf16[128,512]{1,0:T(8,128)(2,1)S(1)} %attend.5), channel_id=1, source_target_pairs={{0,38},{1,35},{2,32},{3,37},{4,34},{5,39},{6,36},{7,33},{8,46},{9,... | collective-permute-start | bytes 393224 | tf_op jit(solution)/shard_map/ppermute | solution.py:204
  79.5 4.6 %attend.6 = bf16[128,512]{1,0:T(8,128)(2,1)S(1)} custom-call(s32[2]{0:T(128)S(1)} %pad_add_fusion.meta, bf16[4,128,512]{2,1,0:T(8,128)(2,1)S(1)} %all-to-all-done.q_ref, bf16[4,4,128,128]{3,2,1,0:T(8,128)(2,1)S(1)} %pad_maximum_fusion.1.own_ref, bf16[4,4,128,128]{3,2,1,0:T(8,128)(2,1)S(1)} %copy-done.1, ...), custom_call_target="tpu_custom_call" | custom-call | flops 1073741824 | bytes 1048576 | tf_op jit(solution)/shard_map/attend/pallas_call | solution.py:125
  84.1 20.3 %collective-permute-start.10 = (bf16[128,512]{1,0:T(8,128)(2,1)S(1)}, bf16[128,512]{1,0:T(8,128)(2,1)S(1)}, u32[]{:S(2)}, u32[]{:S(2)}) collective-permute-start(bf16[128,512]{1,0:T(8,128)(2,1)S(1)} %attend.6), channel_id=1, source_target_pairs={{0,34},{1,39},{2,36},{3,33},{4,38},{5,35},{6,32},{7,37},{8,42},{9,... | collective-permute-start | bytes 393224 | tf_op jit(solution)/shard_map/ppermute | solution.py:204
  104.5 4.6 %attend.7 = bf16[128,512]{1,0:T(8,128)(2,1)S(1)} custom-call(s32[2]{0:T(128)S(1)} %pad_add_fusion.meta, bf16[4,128,512]{2,1,0:T(8,128)(2,1)S(1)} %all-to-all-done.q_ref, bf16[4,4,128,128]{3,2,1,0:T(8,128)(2,1)S(1)} %pad_maximum_fusion.1.own_ref, bf16[4,4,128,128]{3,2,1,0:T(8,128)(2,1)S(1)} %copy-done.1, ...), custom_call_target="tpu_custom_call" | custom-call | flops 1073741824 | bytes 1048576 | tf_op jit(solution)/shard_map/attend/pallas_call | solution.py:125
  109.1 1.9 %collective-permute-start.11 = (bf16[128,512]{1,0:T(8,128)(2,1)S(1)}, bf16[128,512]{1,0:T(8,128)(2,1)S(1)}, u32[]{:S(2)}, u32[]{:S(2)}) collective-permute-start(bf16[128,512]{1,0:T(8,128)(2,1)S(1)} %attend.7), channel_id=1, source_target_pairs={{0,36},{1,37},{2,38},{3,39},{4,32},{5,33},{6,34},{7,35},{8,44},{9,... | collective-permute-start | bytes 393224 | tf_op jit(solution)/shard_map/ppermute | solution.py:204
  111.0 0.0 collective-permute-done.12.hidden_ref
  111.0 0.0 collective-permute-done.9.o1
  111.0 0.0 collective-permute-done.10.o2
  111.1 11.1 %collective-permute-done.11.o3 = bf16[128,512]{1,0:T(8,128)(2,1)S(1)} collective-permute-done((bf16[128,512]{1,0:T(8,128)(2,1)S(1)}, bf16[128,512]{1,0:T(8,128)(2,1)S(1)}, u32[]{:S(2)}, u32[]{:S(2)}) %collective-permute-start.11) | collective-permute-done | bytes 131104 | tf_op jit(solution)/shard_map/ppermute | solution.py:204
  122.1 0.0 collective-permute-done.8.o0
  122.1 1.7 %finish.1 = bf16[1,128,2048]{2,1,0:T(8,128)(2,1)} custom-call(s32[2]{0:T(128)S(1)} %pad_add_fusion.meta, bf16[192,512]{1,0:T(8,128)(2,1)S(1)} %collective-permute-done.8.o0, bf16[128,512]{1,0:T(8,128)(2,1)S(1)} %collective-permute-done.9.o1, bf16[128,512]{1,0:T(8,128)(2,1)S(1)} %collective-permute-done.10.o2, ...), custom_call_target="tpu_custom_call" | custom-call | tf_op jit(solution)/shard_map/finish/pallas_call | solution.py:155
  (18 shorter events, 0.2 us)
Async XLA Ops:
  0.0 0.9 copy-start.4
  0.9 1.0 copy-start.5
  0.9 1.0 copy-start.6
  2.0 17.1 %copy-start.3 = (bf16[1,128,2048]{2,1,0:T(8,128)(2,1)S(1)}, bf16[1,128,2048]{2,1,0:T(8,128)(2,1)}, u32[]{:S(2)}) copy-start(bf16[1,128,2048]{2,1,0:T(8,128)(2,1)} %param.8) | copy-start | bytes 1572868
  2.0 17.7 %collective-permute-start.2 = (bf16[4,128,128]{2,1,0:T(8,128)(2,1)S(1)}, bf16[4,128,128]{2,1,0:T(8,128)(2,1)S(1)}, u32[]{:S(2)}, u32[]{:S(2)}) collective-permute-start(bf16[4,128,128]{2,1,0:T(8,128)(2,1)S(1)} %pad_maximum_fusion.4), channel_id=1, source_target_pairs={{0,4},{1,5},{2,6},{3,7},{4,0},{5,1},{6,2},{7,3},{8,12},{9,13},{10,... | collective-permute-start | bytes 393224 | tf_op jit(solution)/shard_map/ppermute | solution.py:182
  12.2 8.1 %collective-permute-start.1 = (bf16[4,128,128]{2,1,0:T(8,128)(2,1)S(1)}, bf16[4,128,128]{2,1,0:T(8,128)(2,1)S(1)}, u32[]{:S(2)}, u32[]{:S(2)}) collective-permute-start(bf16[4,128,128]{2,1,0:T(8,128)(2,1)S(1)} %pad_maximum_fusion.3), channel_id=1, source_target_pairs={{0,6},{1,3},{2,0},{3,5},{4,2},{5,7},{6,4},{7,1},{8,14},{9,11},{10,... | collective-permute-start | bytes 393224 | tf_op jit(solution)/shard_map/ppermute | solution.py:182
  14.2 10.4 %collective-permute-start = (bf16[4,128,128]{2,1,0:T(8,128)(2,1)S(1)}, bf16[4,128,128]{2,1,0:T(8,128)(2,1)S(1)}, u32[]{:S(2)}, u32[]{:S(2)}) collective-permute-start(bf16[4,128,128]{2,1,0:T(8,128)(2,1)S(1)} %pad_maximum_fusion.2), channel_id=1, source_target_pairs={{0,2},{1,7},{2,4},{3,1},{4,6},{5,3},{6,0},{7,5},{8,10},{9,15},{10,... | collective-permute-start | bytes 393224 | tf_op jit(solution)/shard_map/ppermute | solution.py:182
  24.6 10.9 %copy-start.7 = (bf16[1,2048]{1,0:T(2,128)(2,1)S(1)}, bf16[1,2048]{1,0:T(2,128)(2,1)}, u32[]{:S(2)}) copy-start(bf16[1,2048]{1,0:T(2,128)(2,1)} %param.9) | copy-start | bytes 12292
  24.7 12.6 %collective-permute-start.6 = (bf16[4,2,128,128]{3,2,1,0:T(8,128)(2,1)S(1)}, bf16[4,2,128,128]{3,2,1,0:T(8,128)(2,1)S(1)}, u32[]{:S(2)}, u32[]{:S(2)}) collective-permute-start(bf16[4,2,128,128]{3,2,1,0:T(8,128)(2,1)S(1)} %get-tuple-element.6), channel_id=1, source_target_pairs={{0,16},{1,17},{2,18},{3,19},{4,20},{5,21},{6,22},{7,23},{8,24},{9,... | collective-permute-start | bytes 786440 | tf_op jit(solution)/shard_map/ppermute | solution.py:195
  29.7 11.7 %collective-permute-start.5 = (bf16[4,2,128,128]{3,2,1,0:T(8,128)(2,1)S(1)}, bf16[4,2,128,128]{3,2,1,0:T(8,128)(2,1)S(1)}, u32[]{:S(2)}, u32[]{:S(2)}) collective-permute-start(bf16[4,2,128,128]{3,2,1,0:T(8,128)(2,1)S(1)} %get-tuple-element.7), channel_id=1, source_target_pairs={{0,24},{1,9},{2,26},{3,11},{4,28},{5,13},{6,30},{7,15},{8,0},{9,17... | collective-permute-start | bytes 786440 | tf_op jit(solution)/shard_map/ppermute | solution.py:195
  32.7 9.6 %collective-permute-start.4 = (bf16[4,2,128,128]{3,2,1,0:T(8,128)(2,1)S(1)}, bf16[4,2,128,128]{3,2,1,0:T(8,128)(2,1)}, u32[]{:S(2)}, u32[]{:S(2)}) collective-permute-start(bf16[4,2,128,128]{3,2,1,0:T(8,128)(2,1)S(1)} %get-tuple-element.5), channel_id=1, source_target_pairs={{0,8},{1,25},{2,10},{3,27},{4,12},{5,29},{6,14},{7,31},{8,16},{9,1... | collective-permute-start | bytes 786440 | tf_op jit(solution)/shard_map/ppermute | solution.py:195
  43.4 15.0 %collective-permute-start.7 = (bf16[3,4,2,128,128]{4,3,2,1,0:T(8,128)(2,1)S(1)}, bf16[3,4,2,128,128]{4,3,2,1,0:T(8,128)(2,1)S(1)}, u32[]{:S(2)}, u32[]{:S(2)}) collective-permute-start(bf16[3,4,2,128,128]{4,3,2,1,0:T(8,128)(2,1)S(1)} %pad_maximum_fusion.far_ref), channel_id=1, source_target_pairs={{0,1},{1,0},{2,3},{3,2},{4,5},{5,4},{6,7},{7,6},{8,9},{9,8},{10,11... | collective-permute-start | bytes 2359304 | tf_op jit(solution)/shard_map/ppermute | solution.py:198
  46.2 12.1 %copy-start.2 = (bf16[1,2048]{1,0:T(2,128)(2,1)S(1)}, bf16[1,2048]{1,0:T(2,128)(2,1)}, u32[]{:S(2)}) copy-start(bf16[1,2048]{1,0:T(2,128)(2,1)} %gain_ref.7) | copy-start | bytes 12292
  46.2 22.8 %all-to-all-start = ((bf16[4,128,512]{2,1,0:T(8,128)(2,1)}), bf16[4,128,512]{2,1,0:T(8,128)(2,1)S(1)}, u32[]{:S(2)}, u32[]{:S(2)}) async-start(bf16[4,128,512]{2,1,0:T(8,128)(2,1)} %fusion.q_ref), calls=%async_computation | async-start | bytes 1048576 | tf_op jit(solution)/shard_map/all_to_all | solution.py:189
  52.9 5.4 %collective-permute-start.3 = (bf16[4,4,128,128]{3,2,1,0:T(8,128)(2,1)S(1)}, bf16[4,4,128,128]{3,2,1,0:T(8,128)(2,1)S(1)}, u32[]{:S(2)}, u32[]{:S(2)}) collective-permute-start(bf16[4,4,128,128]{3,2,1,0:T(8,128)(2,1)S(1)} %pad_maximum_fusion.1.own_ref), channel_id=1, source_target_pairs={{0,1},{1,0},{2,3},{3,2},{4,5},{5,4},{6,7},{7,6},{8,9},{9,8},{10,11... | collective-permute-start | bytes 1572872 | tf_op jit(solution)/shard_map/ppermute | solution.py:196
  55.0 56.0 %collective-permute-start.12 = (bf16[1,128,2048]{2,1,0:T(8,128)(2,1)}, bf16[1,128,2048]{2,1,0:T(8,128)(2,1)S(1)}, u32[]{:S(2)}, u32[]{:S(2)}) collective-permute-start(bf16[1,128,2048]{2,1,0:T(8,128)(2,1)} %param.8), channel_id=1, source_target_pairs={{0,32},{32,64},{64,96},{96,128},{128,160},{160,192},{192,224},{224... | collective-permute-start | bytes 1572872 | tf_op jit(solution)/shard_map/ppermute | solution.py:179
  58.3 5.4 %copy-start = (bf16[4,4,128,128]{3,2,1,0:T(8,128)(2,1)}, bf16[4,4,128,128]{3,2,1,0:T(8,128)(2,1)S(1)}, u32[]{:S(2)}) copy-start(bf16[4,4,128,128]{3,2,1,0:T(8,128)(2,1)S(1)} %collective-permute-done.3.other_ref) | copy-start | bytes 1572868
  63.7 58.4 %collective-permute-start.8 = (bf16[192,512]{1,0:T(8,128)(2,1)S(1)}, bf16[192,512]{1,0:T(8,128)(2,1)S(1)}, u32[]{:S(2)}, u32[]{:S(2)}) collective-permute-start(bf16[192,512]{1,0:T(8,128)(2,1)S(1)} %attend.4), channel_id=1, source_target_pairs={{0,32},{1,33},{2,34},{3,35},{4,36},{5,37},{6,38},{7,39},{8,40},{9,... | collective-permute-start | bytes 589832 | tf_op jit(solution)/shard_map/ppermute | solution.py:204
  69.1 1.0 copy-start.1
  74.7 36.3 %collective-permute-start.9 = (bf16[128,512]{1,0:T(8,128)(2,1)S(1)}, bf16[128,512]{1,0:T(8,128)(2,1)S(1)}, u32[]{:S(2)}, u32[]{:S(2)}) collective-permute-start(bf16[128,512]{1,0:T(8,128)(2,1)S(1)} %attend.5), channel_id=1, source_target_pairs={{0,38},{1,35},{2,32},{3,37},{4,34},{5,39},{6,36},{7,33},{8,46},{9,... | collective-permute-start | bytes 393224 | tf_op jit(solution)/shard_map/ppermute | solution.py:204
  84.1 26.9 %collective-permute-start.10 = (bf16[128,512]{1,0:T(8,128)(2,1)S(1)}, bf16[128,512]{1,0:T(8,128)(2,1)S(1)}, u32[]{:S(2)}, u32[]{:S(2)}) collective-permute-start(bf16[128,512]{1,0:T(8,128)(2,1)S(1)} %attend.6), channel_id=1, source_target_pairs={{0,34},{1,39},{2,36},{3,33},{4,38},{5,35},{6,32},{7,37},{8,42},{9,... | collective-permute-start | bytes 393224 | tf_op jit(solution)/shard_map/ppermute | solution.py:204
  109.1 13.0 %collective-permute-start.11 = (bf16[128,512]{1,0:T(8,128)(2,1)S(1)}, bf16[128,512]{1,0:T(8,128)(2,1)S(1)}, u32[]{:S(2)}, u32[]{:S(2)}) collective-permute-start(bf16[128,512]{1,0:T(8,128)(2,1)S(1)} %attend.7), channel_id=1, source_target_pairs={{0,36},{1,37},{2,38},{3,39},{4,32},{5,33},{6,34},{7,35},{8,44},{9,... | collective-permute-start | bytes 393224 | tf_op jit(solution)/shard_map/ppermute | solution.py:204
where the time goes:
time: 125 us; the launch traced here: 124 us
  starting transfers between devices  70.3 us (56%)
  waiting for transfers between devices  25.4 us (20%)
  Pallas kernels  20.9 us (17%)
  local copies, waits for them, and re-layouts  3.61 us (3%)
  other arithmetic  2.54 us (2%)
    ppermute x4, starting transfers between devices, on_device(): parts[k] = lax.ppermute(attended, ('section', 'seq'), home_pairs(ROUNDS[k]))  29.4 us
    pallas_call x4, Pallas kernels, attend(): pl.pallas_call(functools.partial(attention_kernel, kq=kq), out_shape=jax....  19.2 us
    ppermute x3, starting transfers between devices, on_device(): pieces.append(lax.ppermute(kv_of((z + sg * r) % 4), 'seq', along_z(r)))  16.9 us
    ppermute x4, waiting for transfers between devices, on_device(): parts[k] = lax.ppermute(attended, ('section', 'seq'), home_pairs(ROUNDS[k]))  11.1 us
    ppermute x3, starting transfers between devices, on_device(): far.append(lax.ppermute(picked, 'seq', along_x(r)))  10.8 us
    all_to_all x1, starting transfers between devices, on_device(): gathered = lax.all_to_all(by_group, 'seq', 0, 0, axis_index_groups=Z_GROUPS)  6.65 us
    ppermute x3, waiting for transfers between devices, on_device(): far.append(lax.ppermute(picked, 'seq', along_x(r)))  6.49 us
    ppermute x3, waiting for transfers between devices, on_device(): pieces.append(lax.ppermute(kv_of((z + sg * r) % 4), 'seq', along_z(r)))  4.85 us
  transfers between devices with their start and end apart: 14, of which 7 were waited for; matrix products, arithmetic and copies ran while one was open for 2% of the time, Pallas kernels for 16%

commit v1 on v0

--- a/solution.py
+++ b/solution.py
@@ -52,7 +52,6 @@
     ]
 
 
-Z_GROUPS = [[seq_of(x, z, c) for z in range(ZS)] for x in range(XS) for c in range(2)]
 OTHER_CORE = [(q, q ^ 1) for q in range(SEQ)]
 
 
@@ -70,7 +69,6 @@
     place = [[2 * ((z - flip * r + 4) % 4) + core for r in ROUNDS] for flip, core in ((sg, c), (-sg, 1 - c))]
     diag = place[0][kq]
     heads = TILE // BLK
-    q_at = z if kq == 0 else (z - sg * ROUNDS[kq] + 4) % 4
     blocks = []
     for half, ref in ((0, far_ref), (1, far_other_ref)):
         flip = -sg if half else sg
@@ -91,8 +89,7 @@
     blocks.append((own_ref, (kq, 2), (kq, 3), (cols > rows) & (cols >= limit - (row_base + diag * BLK))))
     pairs = [blocks[j : j + 2] for j in range(0, len(blocks), 2)]
     for t in range(GROUP // heads):
-        lanes = [slice((t * heads + h) * BLK, (t * heads + h + 1) * BLK) for h in range(heads)]
-        q = jnp.concatenate([q_ref[q_at, :, lane] for lane in lanes], 0)
+        q = jnp.concatenate([q_ref[:, (t * heads + h) * BLK : (t * heads + h + 1) * BLK] for h in range(heads)], 0)
         best = None
         for j, pair in enumerate(pairs):
             scores = nt(q, jnp.concatenate([ref[k_at] for ref, k_at, _, _ in pair], 0))
@@ -185,8 +182,13 @@
     widened = hidden[0].astype(jnp.float32)
     scale = lax.rsqrt(jnp.mean(widened * widened, axis=-1, keepdims=True) + 1e-06)
     queries = (widened * scale * query_gain[0].astype(jnp.float32)).astype(jnp.bfloat16)
-    by_group = jnp.transpose(queries.reshape(BLK, KV_HEADS, GROUP * HEAD), (1, 0, 2))
-    gathered = lax.all_to_all(by_group, "seq", 0, 0, axis_index_groups=Z_GROUPS)
+
+    def q_of(head):
+        return lax.dynamic_slice(queries, (0, head * GROUP * HEAD), (BLK, GROUP * HEAD))
+
+    qs = [q_of(z)]
+    for k, r in enumerate(ROUNDS[1:], 1):
+        qs.append(lax.ppermute(q_of((z + sg * r) % 4), "seq", along_z(r)))
 
     far = []
     for k, r in enumerate(ROUNDS[1:], 1):
@@ -199,8 +201,8 @@
 
     meta = jnp.stack([limit, me])
     parts = [None] * 4
-    for k in (0, 3, 1, 2):
-        attended = attend(meta, gathered if k else by_group, own, other, far, far_other, k, out_gain)
+    for k in (3, 1, 2, 0):
+        attended = attend(meta, qs[k], own, other, far, far_other, k, out_gain)
         parts[k] = lax.ppermute(attended, ("section", "seq"), home_pairs(ROUNDS[k]))
     return finish(meta, parts, hidden_before)
 

time: 125 us -> 112 us (0.90)
  the two profiles are of different devices: /device:TPU:112 before, /device:TPU:8 now
where the time goes in v1:
time: 112 us
  starting transfers between devices  67.8 us (61%)
  Pallas kernels  20.3 us (18%)
  waiting for transfers between devices  18.9 us (17%)
  local copies, waits for them, and re-layouts  2.8 us (2%)
    pallas_call x4, Pallas kernels, attend(): pl.pallas_call(functools.partial(attention_kernel, kq=kq), out_shape=jax....  18.6 us
    ppermute x3, starting transfers between devices, on_device(): pieces.append(lax.ppermute(kv_of((z + sg * r) % 4), 'seq', along_z(r)))  17.7 us
    ppermute x4, starting transfers between devices, on_device(): parts[k] = lax.ppermute(attended, ('section', 'seq'), home_pairs(ROUNDS[k]))  16.3 us
    ppermute x3, starting transfers between devices, on_device(): qs.append(lax.ppermute(q_of((z + sg * r) % 4), 'seq', along_z(r)))  15.2 us
    ppermute x3, starting transfers between devices, on_device(): far.append(lax.ppermute(picked, 'seq', along_x(r)))  10.9 us
    ppermute x4, waiting for transfers between devices, on_device(): parts[k] = lax.ppermute(attended, ('section', 'seq'), home_pairs(ROUNDS[k]))  9.82 us
    ppermute x3, waiting for transfers between devices, on_device(): pieces.append(lax.ppermute(kv_of((z + sg * r) % 4), 'seq', along_z(r)))  6.07 us
    ppermute x1, starting transfers between devices, on_device(): lax.ppermute(hidden, 'section', [(s, (s + 1) % SECTIONS) for s in range(S...  3.48 us
  transfers between devices with their start and end apart: 16, of which 4 were waited for; matrix products, arithmetic and copies ran while one was open for 1% of the time, Pallas kernels for 17%

profile of v1, /device:TPU:8, one launch (start us, length us, event | category | flops | bytes accessed | tf_op | source)
XLA Modules:
  0.0 111.6 jit_solution(5695325820256806526)
XLA Ops:
  0.0 0.9 copy-done.2
  0.9 0.9 constant_dynamic-slice_fusion.18
  1.8 0.1 copy-done.3
  1.9 0.1 copy-done.4
  2.0 10.9 %collective-permute-start.2 = (bf16[4,128,128]{2,1,0:T(8,128)(2,1)S(1)}, bf16[4,128,128]{2,1,0:T(8,128)(2,1)S(1)}, u32[]{:S(2)}, u32[]{:S(2)}) collective-permute-start(bf16[4,128,128]{2,1,0:T(8,128)(2,1)S(1)} %pad_maximum_fusion.4), channel_id=1, source_target_pairs={{0,4},{1,5},{2,6},{3,7},{4,0},{5,1},{6,2},{7,3},{8,12},{9,13},{10,... | collective-permute-start | bytes 393224 | tf_op jit(solution)/shard_map/ppermute | solution.py:179
  13.0 1.9 %collective-permute-start.1 = (bf16[4,128,128]{2,1,0:T(8,128)(2,1)S(1)}, bf16[4,128,128]{2,1,0:T(8,128)(2,1)S(1)}, u32[]{:S(2)}, u32[]{:S(2)}) collective-permute-start(bf16[4,128,128]{2,1,0:T(8,128)(2,1)S(1)} %pad_maximum_fusion.3), channel_id=1, source_target_pairs={{0,6},{1,3},{2,0},{3,5},{4,2},{5,7},{6,4},{7,1},{8,14},{9,11},{10,... | collective-permute-start | bytes 393224 | tf_op jit(solution)/shard_map/ppermute | solution.py:179
  14.9 4.8 %collective-permute-start = (bf16[4,128,128]{2,1,0:T(8,128)(2,1)S(1)}, bf16[4,128,128]{2,1,0:T(8,128)(2,1)S(1)}, u32[]{:S(2)}, u32[]{:S(2)}) collective-permute-start(bf16[4,128,128]{2,1,0:T(8,128)(2,1)S(1)} %pad_maximum_fusion.2), channel_id=1, source_target_pairs={{0,2},{1,7},{2,4},{3,1},{4,6},{5,3},{6,0},{7,5},{8,10},{9,15},{10,... | collective-permute-start | bytes 393224 | tf_op jit(solution)/shard_map/ppermute | solution.py:179
  19.9 0.0 collective-permute-done.2
  19.9 6.1 %collective-permute-done.1 = bf16[4,128,128]{2,1,0:T(8,128)(2,1)S(1)} collective-permute-done((bf16[4,128,128]{2,1,0:T(8,128)(2,1)S(1)}, bf16[4,128,128]{2,1,0:T(8,128)(2,1)S(1)}, u32[]{:S(2)}, u32[]{:S(2)}) %collective-permute-start.1) | collective-permute-done | bytes 131104 | tf_op jit(solution)/shard_map/ppermute | solution.py:179
  25.9 0.0 collective-permute-done
  25.9 0.1 pad_maximum_fusion.1.own_ref
  26.0 0.0 copy-start.1
  26.0 0.1 constant_dynamic-slice_fusion.5
  26.1 5.1 %collective-permute-start.6 = (bf16[4,2,128,128]{3,2,1,0:T(8,128)(2,1)S(1)}, bf16[4,2,128,128]{3,2,1,0:T(8,128)(2,1)S(1)}, u32[]{:S(2)}, u32[]{:S(2)}) collective-permute-start(bf16[4,2,128,128]{3,2,1,0:T(8,128)(2,1)S(1)} %get-tuple-element.10), channel_id=1, source_target_pairs={{0,16},{1,17},{2,18},{3,19},{4,20},{5,21},{6,22},{7,23},{8,24},{9,... | collective-permute-start | bytes 786440 | tf_op jit(solution)/shard_map/ppermute | solution.py:197
  31.2 3.0 %collective-permute-start.5 = (bf16[4,2,128,128]{3,2,1,0:T(8,128)(2,1)S(1)}, bf16[4,2,128,128]{3,2,1,0:T(8,128)(2,1)S(1)}, u32[]{:S(2)}, u32[]{:S(2)}) collective-permute-start(bf16[4,2,128,128]{3,2,1,0:T(8,128)(2,1)S(1)} %get-tuple-element.11), channel_id=1, source_target_pairs={{0,24},{1,9},{2,26},{3,11},{4,28},{5,13},{6,30},{7,15},{8,0},{9,17... | collective-permute-start | bytes 786440 | tf_op jit(solution)/shard_map/ppermute | solution.py:197
  34.2 2.8 %collective-permute-start.4 = (bf16[4,2,128,128]{3,2,1,0:T(8,128)(2,1)S(1)}, bf16[4,2,128,128]{3,2,1,0:T(8,128)(2,1)S(1)}, u32[]{:S(2)}, u32[]{:S(2)}) collective-permute-start(bf16[4,2,128,128]{3,2,1,0:T(8,128)(2,1)S(1)} %get-tuple-element.9), channel_id=1, source_target_pairs={{0,8},{1,25},{2,10},{3,27},{4,12},{5,29},{6,14},{7,31},{8,16},{9,1... | collective-permute-start | bytes 786440 | tf_op jit(solution)/shard_map/ppermute | solution.py:197
  37.1 3.5 %collective-permute-start.15 = (bf16[1,128,2048]{2,1,0:T(8,128)(2,1)S(1)}, bf16[1,128,2048]{2,1,0:T(8,128)(2,1)S(1)}, u32[]{:S(2)}, u32[]{:S(2)}) collective-permute-start(bf16[1,128,2048]{2,1,0:T(8,128)(2,1)S(1)} %copy-done.1), channel_id=1, source_target_pairs={{0,32},{32,64},{64,96},{96,128},{128,160},{160,192},{192,224},{224... | collective-permute-start | bytes 1572872 | tf_op jit(solution)/shard_map/ppermute | solution.py:176
  40.5 0.2 fusion
  40.7 0.0 collective-permute-done.6
  40.7 2.8 %collective-permute-done.5 = bf16[4,2,128,128]{3,2,1,0:T(8,128)(2,1)S(1)} collective-permute-done((bf16[4,2,128,128]{3,2,1,0:T(8,128)(2,1)S(1)}, bf16[4,2,128,128]{3,2,1,0:T(8,128)(2,1)S(1)}, u32[]{:S(2)}, u32[]{:S(2)}) %collective-permute-start.5) | collective-permute-done | bytes 262176 | tf_op jit(solution)/shard_map/ppermute | solution.py:197
  43.6 0.1 collective-permute-done.4
  43.7 0.1 pad_maximum_fusion.far_ref
  43.8 1.9 %collective-permute-start.7 = (bf16[3,4,2,128,128]{4,3,2,1,0:T(8,128)(2,1)S(1)}, bf16[3,4,2,128,128]{4,3,2,1,0:T(8,128)(2,1)S(1)}, u32[]{:S(2)}, u32[]{:S(2)}) collective-permute-start(bf16[3,4,2,128,128]{4,3,2,1,0:T(8,128)(2,1)S(1)} %pad_maximum_fusion.far_ref), channel_id=1, source_target_pairs={{0,1},{1,0},{2,3},{3,2},{4,5},{5,4},{6,7},{7,6},{8,9},{9,8},{10,11... | collective-permute-start | bytes 2359304 | tf_op jit(solution)/shard_map/ppermute | solution.py:200
  45.8 0.0 copy-start.5
  45.8 0.7 copy-done.5
  46.5 2.4 %collective-permute-start.3 = (bf16[4,4,128,128]{3,2,1,0:T(8,128)(2,1)S(1)}, bf16[4,4,128,128]{3,2,1,0:T(8,128)(2,1)S(1)}, u32[]{:S(2)}, u32[]{:S(2)}) collective-permute-start(bf16[4,4,128,128]{3,2,1,0:T(8,128)(2,1)S(1)} %pad_maximum_fusion.1.own_ref), channel_id=1, source_target_pairs={{0,1},{1,0},{2,3},{3,2},{4,5},{5,4},{6,7},{7,6},{8,9},{9,8},{10,11... | collective-permute-start | bytes 1572872 | tf_op jit(solution)/shard_map/ppermute | solution.py:198
  48.9 0.2 fusion.2
  49.2 0.0 copy-start
  49.2 3.7 %collective-permute-start.9 = (bf16[128,512]{1,0:T(8,128)(2,1)S(1)}, bf16[128,512]{1,0:T(8,128)(2,1)S(1)}, u32[]{:S(2)}, u32[]{:S(2)}) collective-permute-start(bf16[128,512]{1,0:T(8,128)(2,1)S(1)} %get-tuple-element.7), channel_id=1, source_target_pairs={{0,2},{1,7},{2,4},{3,1},{4,6},{5,3},{6,0},{7,5},{8,10},{9,15},{10,... | collective-permute-start | bytes 393224 | tf_op jit(solution)/shard_map/ppermute | solution.py:191
  52.9 4.2 %collective-permute-start.11 = (bf16[128,512]{1,0:T(8,128)(2,1)S(1)}, bf16[128,512]{1,0:T(8,128)(2,1)S(1)}, u32[]{:S(2)}, u32[]{:S(2)}) collective-permute-start(bf16[128,512]{1,0:T(8,128)(2,1)S(1)} %get-tuple-element.6), channel_id=1, source_target_pairs={{0,6},{1,3},{2,0},{3,5},{4,2},{5,7},{6,4},{7,1},{8,14},{9,11},{10,... | collective-permute-start | bytes 393224 | tf_op jit(solution)/shard_map/ppermute | solution.py:191
  57.8 0.1 pad_add_fusion.meta
  57.9 0.0 collective-permute-done.3.other_ref
  57.9 7.2 %collective-permute-start.13 = (bf16[128,512]{1,0:T(8,128)(2,1)S(1)}, bf16[128,512]{1,0:T(8,128)(2,1)S(1)}, u32[]{:S(2)}, u32[]{:S(2)}) collective-permute-start(bf16[128,512]{1,0:T(8,128)(2,1)S(1)} %get-tuple-element.5), channel_id=1, source_target_pairs={{0,4},{1,5},{2,6},{3,7},{4,0},{5,1},{6,2},{7,3},{8,12},{9,13},{10,... | collective-permute-start | bytes 393224 | tf_op jit(solution)/shard_map/ppermute | solution.py:191
  65.1 0.0 collective-permute-done.7.far_other_ref
  65.1 4.7 %attend.4 = bf16[192,512]{1,0:T(8,128)(2,1)S(1)} custom-call(s32[2]{0:T(128)S(1)} %pad_add_fusion.meta, bf16[128,512]{1,0:T(8,128)(2,1)S(1)} %get-tuple-element.8.q_ref, bf16[4,4,128,128]{3,2,1,0:T(8,128)(2,1)S(1)} %pad_maximum_fusion.1.own_ref, bf16[4,4,128,128]{3,2,1,0:T(8,128)(2,1)S(1)} %collective-permute-done.3.other_ref, ...), custom_call_target="tpu_custom_call" | custom-call | flops 1073741824 | bytes 1048576 | tf_op jit(solution)/shard_map/attend/pallas_call | solution.py:122
  69.8 3.5 %collective-permute-start.8 = (bf16[192,512]{1,0:T(8,128)(2,1)S(1)}, bf16[192,512]{1,0:T(8,128)(2,1)S(1)}, u32[]{:S(2)}, u32[]{:S(2)}) collective-permute-start(bf16[192,512]{1,0:T(8,128)(2,1)S(1)} %attend.4), channel_id=1, source_target_pairs={{0,32},{1,33},{2,34},{3,35},{4,36},{5,37},{6,38},{7,39},{8,40},{9,... | collective-permute-start | bytes 589832 | tf_op jit(solution)/shard_map/ppermute | solution.py:206
  73.3 0.0 collective-permute-done.9.q_ref
  73.3 4.7 %attend.5 = bf16[128,512]{1,0:T(8,128)(2,1)S(1)} custom-call(s32[2]{0:T(128)S(1)} %pad_add_fusion.meta, bf16[128,512]{1,0:T(8,128)(2,1)S(1)} %collective-permute-done.9.q_ref, bf16[4,4,128,128]{3,2,1,0:T(8,128)(2,1)S(1)} %pad_maximum_fusion.1.own_ref, bf16[4,4,128,128]{3,2,1,0:T(8,128)(2,1)S(1)} %collective-permute-done.3.other_ref, ...), custom_call_target="tpu_custom_call" | custom-call | flops 1073741824 | bytes 1048576 | tf_op jit(solution)/shard_map/attend/pallas_call | solution.py:122
  78.0 3.1 %collective-permute-start.10 = (bf16[128,512]{1,0:T(8,128)(2,1)S(1)}, bf16[128,512]{1,0:T(8,128)(2,1)S(1)}, u32[]{:S(2)}, u32[]{:S(2)}) collective-permute-start(bf16[128,512]{1,0:T(8,128)(2,1)S(1)} %attend.5), channel_id=1, source_target_pairs={{0,38},{1,35},{2,32},{3,37},{4,34},{5,39},{6,36},{7,33},{8,46},{9,... | collective-permute-start | bytes 393224 | tf_op jit(solution)/shard_map/ppermute | solution.py:206
  81.1 0.0 collective-permute-done.11.q_ref
  81.1 4.7 %attend.6 = bf16[128,512]{1,0:T(8,128)(2,1)S(1)} custom-call(s32[2]{0:T(128)S(1)} %pad_add_fusion.meta, bf16[128,512]{1,0:T(8,128)(2,1)S(1)} %collective-permute-done.11.q_ref, bf16[4,4,128,128]{3,2,1,0:T(8,128)(2,1)S(1)} %pad_maximum_fusion.1.own_ref, bf16[4,4,128,128]{3,2,1,0:T(8,128)(2,1)S(1)} %collective-permute-done.3.other_ref, ...), custom_call_target="tpu_custom_call" | custom-call | flops 1073741824 | bytes 1048576 | tf_op jit(solution)/shard_map/attend/pallas_call | solution.py:122
  85.8 7.0 %collective-permute-start.12 = (bf16[128,512]{1,0:T(8,128)(2,1)S(1)}, bf16[128,512]{1,0:T(8,128)(2,1)S(1)}, u32[]{:S(2)}, u32[]{:S(2)}) collective-permute-start(bf16[128,512]{1,0:T(8,128)(2,1)S(1)} %attend.6), channel_id=1, source_target_pairs={{0,34},{1,39},{2,36},{3,33},{4,38},{5,35},{6,32},{7,37},{8,42},{9,... | collective-permute-start | bytes 393224 | tf_op jit(solution)/shard_map/ppermute | solution.py:206
  92.9 4.6 %attend.7 = bf16[128,512]{1,0:T(8,128)(2,1)S(1)} custom-call(s32[2]{0:T(128)S(1)} %pad_add_fusion.meta, bf16[128,512]{1,0:T(8,128)(2,1)S(1)} %collective-permute-done.13.q_ref, bf16[4,4,128,128]{3,2,1,0:T(8,128)(2,1)S(1)} %pad_maximum_fusion.1.own_ref, bf16[4,4,128,128]{3,2,1,0:T(8,128)(2,1)S(1)} %collective-permute-done.3.other_ref, ...), custom_call_target="tpu_custom_call" | custom-call | flops 1073741824 | bytes 1048576 | tf_op jit(solution)/shard_map/attend/pallas_call | solution.py:122
  97.5 2.6 %collective-permute-start.14 = (bf16[128,512]{1,0:T(8,128)(2,1)S(1)}, bf16[128,512]{1,0:T(8,128)(2,1)S(1)}, u32[]{:S(2)}, u32[]{:S(2)}) collective-permute-start(bf16[128,512]{1,0:T(8,128)(2,1)S(1)} %attend.7), channel_id=1, source_target_pairs={{0,36},{1,37},{2,38},{3,39},{4,32},{5,33},{6,34},{7,35},{8,44},{9,... | collective-permute-start | bytes 393224 | tf_op jit(solution)/shard_map/ppermute | solution.py:206
  100.1 0.0 collective-permute-done.10.o1
  100.1 0.0 collective-permute-done.12.o2
  100.1 9.8 %collective-permute-done.14.o3 = bf16[128,512]{1,0:T(8,128)(2,1)S(1)} collective-permute-done((bf16[128,512]{1,0:T(8,128)(2,1)S(1)}, bf16[128,512]{1,0:T(8,128)(2,1)S(1)}, u32[]{:S(2)}, u32[]{:S(2)}) %collective-permute-start.14) | collective-permute-done | bytes 131104 | tf_op jit(solution)/shard_map/ppermute | solution.py:206
  110.0 1.7 %finish.1 = bf16[1,128,2048]{2,1,0:T(8,128)(2,1)} custom-call(s32[2]{0:T(128)S(1)} %pad_add_fusion.meta, bf16[192,512]{1,0:T(8,128)(2,1)S(1)} %collective-permute-done.8.o0, bf16[128,512]{1,0:T(8,128)(2,1)S(1)} %collective-permute-done.10.o1, bf16[128,512]{1,0:T(8,128)(2,1)S(1)} %collective-permute-done.12.o2, ...), custom_call_target="tpu_custom_call" | custom-call | tf_op jit(solution)/shard_map/finish/pallas_call | solution.py:152
  (16 shorter events, 0.2 us)
Async XLA Ops:
  0.0 0.9 copy-start.2
  0.9 1.0 copy-start.3
  0.9 1.0 copy-start.4
  2.0 17.8 %collective-permute-start.2 = (bf16[4,128,128]{2,1,0:T(8,128)(2,1)S(1)}, bf16[4,128,128]{2,1,0:T(8,128)(2,1)S(1)}, u32[]{:S(2)}, u32[]{:S(2)}) collective-permute-start(bf16[4,128,128]{2,1,0:T(8,128)(2,1)S(1)} %pad_maximum_fusion.4), channel_id=1, source_target_pairs={{0,4},{1,5},{2,6},{3,7},{4,0},{5,1},{6,2},{7,3},{8,12},{9,13},{10,... | collective-permute-start | bytes 393224 | tf_op jit(solution)/shard_map/ppermute | solution.py:179
  13.0 13.0 %collective-permute-start.1 = (bf16[4,128,128]{2,1,0:T(8,128)(2,1)S(1)}, bf16[4,128,128]{2,1,0:T(8,128)(2,1)S(1)}, u32[]{:S(2)}, u32[]{:S(2)}) collective-permute-start(bf16[4,128,128]{2,1,0:T(8,128)(2,1)S(1)} %pad_maximum_fusion.3), channel_id=1, source_target_pairs={{0,6},{1,3},{2,0},{3,5},{4,2},{5,7},{6,4},{7,1},{8,14},{9,11},{10,... | collective-permute-start | bytes 393224 | tf_op jit(solution)/shard_map/ppermute | solution.py:179
  14.9 11.0 %collective-permute-start = (bf16[4,128,128]{2,1,0:T(8,128)(2,1)S(1)}, bf16[4,128,128]{2,1,0:T(8,128)(2,1)S(1)}, u32[]{:S(2)}, u32[]{:S(2)}) collective-permute-start(bf16[4,128,128]{2,1,0:T(8,128)(2,1)S(1)} %pad_maximum_fusion.2), channel_id=1, source_target_pairs={{0,2},{1,7},{2,4},{3,1},{4,6},{5,3},{6,0},{7,5},{8,10},{9,15},{10,... | collective-permute-start | bytes 393224 | tf_op jit(solution)/shard_map/ppermute | solution.py:179
  26.0 11.0 %copy-start.1 = (bf16[1,128,2048]{2,1,0:T(8,128)(2,1)S(1)}, bf16[1,128,2048]{2,1,0:T(8,128)(2,1)}, u32[]{:S(2)}) copy-start(bf16[1,128,2048]{2,1,0:T(8,128)(2,1)} %param.8) | copy-start | bytes 1572868
  26.1 14.6 %collective-permute-start.6 = (bf16[4,2,128,128]{3,2,1,0:T(8,128)(2,1)S(1)}, bf16[4,2,128,128]{3,2,1,0:T(8,128)(2,1)S(1)}, u32[]{:S(2)}, u32[]{:S(2)}) collective-permute-start(bf16[4,2,128,128]{3,2,1,0:T(8,128)(2,1)S(1)} %get-tuple-element.10), channel_id=1, source_target_pairs={{0,16},{1,17},{2,18},{3,19},{4,20},{5,21},{6,22},{7,23},{8,24},{9,... | collective-permute-start | bytes 786440 | tf_op jit(solution)/shard_map/ppermute | solution.py:197
  31.2 12.4 %collective-permute-start.5 = (bf16[4,2,128,128]{3,2,1,0:T(8,128)(2,1)S(1)}, bf16[4,2,128,128]{3,2,1,0:T(8,128)(2,1)S(1)}, u32[]{:S(2)}, u32[]{:S(2)}) collective-permute-start(bf16[4,2,128,128]{3,2,1,0:T(8,128)(2,1)S(1)} %get-tuple-element.11), channel_id=1, source_target_pairs={{0,24},{1,9},{2,26},{3,11},{4,28},{5,13},{6,30},{7,15},{8,0},{9,17... | collective-permute-start | bytes 786440 | tf_op jit(solution)/shard_map/ppermute | solution.py:197
  34.2 9.5 %collective-permute-start.4 = (bf16[4,2,128,128]{3,2,1,0:T(8,128)(2,1)S(1)}, bf16[4,2,128,128]{3,2,1,0:T(8,128)(2,1)S(1)}, u32[]{:S(2)}, u32[]{:S(2)}) collective-permute-start(bf16[4,2,128,128]{3,2,1,0:T(8,128)(2,1)S(1)} %get-tuple-element.9), channel_id=1, source_target_pairs={{0,8},{1,25},{2,10},{3,27},{4,12},{5,29},{6,14},{7,31},{8,16},{9,1... | collective-permute-start | bytes 786440 | tf_op jit(solution)/shard_map/ppermute | solution.py:197
  37.1 63.1 %collective-permute-start.15 = (bf16[1,128,2048]{2,1,0:T(8,128)(2,1)S(1)}, bf16[1,128,2048]{2,1,0:T(8,128)(2,1)S(1)}, u32[]{:S(2)}, u32[]{:S(2)}) collective-permute-start(bf16[1,128,2048]{2,1,0:T(8,128)(2,1)S(1)} %copy-done.1), channel_id=1, source_target_pairs={{0,32},{32,64},{64,96},{96,128},{128,160},{160,192},{192,224},{224... | collective-permute-start | bytes 1572872 | tf_op jit(solution)/shard_map/ppermute | solution.py:176
  43.8 21.3 %collective-permute-start.7 = (bf16[3,4,2,128,128]{4,3,2,1,0:T(8,128)(2,1)S(1)}, bf16[3,4,2,128,128]{4,3,2,1,0:T(8,128)(2,1)S(1)}, u32[]{:S(2)}, u32[]{:S(2)}) collective-permute-start(bf16[3,4,2,128,128]{4,3,2,1,0:T(8,128)(2,1)S(1)} %pad_maximum_fusion.far_ref), channel_id=1, source_target_pairs={{0,1},{1,0},{2,3},{3,2},{4,5},{5,4},{6,7},{7,6},{8,9},{9,8},{10,11... | collective-permute-start | bytes 2359304 | tf_op jit(solution)/shard_map/ppermute | solution.py:200
  45.8 0.7 copy-start.5
  46.5 11.4 %collective-permute-start.3 = (bf16[4,4,128,128]{3,2,1,0:T(8,128)(2,1)S(1)}, bf16[4,4,128,128]{3,2,1,0:T(8,128)(2,1)S(1)}, u32[]{:S(2)}, u32[]{:S(2)}) collective-permute-start(bf16[4,4,128,128]{3,2,1,0:T(8,128)(2,1)S(1)} %pad_maximum_fusion.1.own_ref), channel_id=1, source_target_pairs={{0,1},{1,0},{2,3},{3,2},{4,5},{5,4},{6,7},{7,6},{8,9},{9,8},{10,11... | collective-permute-start | bytes 1572872 | tf_op jit(solution)/shard_map/ppermute | solution.py:198
  49.2 16.0 %copy-start = (bf16[1,2048]{1,0:T(2,128)(2,1)S(1)}, bf16[1,2048]{1,0:T(2,128)(2,1)}, u32[]{:S(2)}) copy-start(bf16[1,2048]{1,0:T(2,128)(2,1)} %gain_ref.7) | copy-start | bytes 12292
  49.2 24.1 %collective-permute-start.9 = (bf16[128,512]{1,0:T(8,128)(2,1)S(1)}, bf16[128,512]{1,0:T(8,128)(2,1)S(1)}, u32[]{:S(2)}, u32[]{:S(2)}) collective-permute-start(bf16[128,512]{1,0:T(8,128)(2,1)S(1)} %get-tuple-element.7), channel_id=1, source_target_pairs={{0,2},{1,7},{2,4},{3,1},{4,6},{5,3},{6,0},{7,5},{8,10},{9,15},{10,... | collective-permute-start | bytes 393224 | tf_op jit(solution)/shard_map/ppermute | solution.py:191
  52.9 28.2 %collective-permute-start.11 = (bf16[128,512]{1,0:T(8,128)(2,1)S(1)}, bf16[128,512]{1,0:T(8,128)(2,1)S(1)}, u32[]{:S(2)}, u32[]{:S(2)}) collective-permute-start(bf16[128,512]{1,0:T(8,128)(2,1)S(1)} %get-tuple-element.6), channel_id=1, source_target_pairs={{0,6},{1,3},{2,0},{3,5},{4,2},{5,7},{6,4},{7,1},{8,14},{9,11},{10,... | collective-permute-start | bytes 393224 | tf_op jit(solution)/shard_map/ppermute | solution.py:191
  57.9 35.0 %collective-permute-start.13 = (bf16[128,512]{1,0:T(8,128)(2,1)S(1)}, bf16[128,512]{1,0:T(8,128)(2,1)S(1)}, u32[]{:S(2)}, u32[]{:S(2)}) collective-permute-start(bf16[128,512]{1,0:T(8,128)(2,1)S(1)} %get-tuple-element.5), channel_id=1, source_target_pairs={{0,4},{1,5},{2,6},{3,7},{4,0},{5,1},{6,2},{7,3},{8,12},{9,13},{10,... | collective-permute-start | bytes 393224 | tf_op jit(solution)/shard_map/ppermute | solution.py:191
  69.8 40.1 %collective-permute-start.8 = (bf16[192,512]{1,0:T(8,128)(2,1)S(1)}, bf16[192,512]{1,0:T(8,128)(2,1)S(1)}, u32[]{:S(2)}, u32[]{:S(2)}) collective-permute-start(bf16[192,512]{1,0:T(8,128)(2,1)S(1)} %attend.4), channel_id=1, source_target_pairs={{0,32},{1,33},{2,34},{3,35},{4,36},{5,37},{6,38},{7,39},{8,40},{9,... | collective-permute-start | bytes 589832 | tf_op jit(solution)/shard_map/ppermute | solution.py:206
  78.0 22.1 %collective-permute-start.10 = (bf16[128,512]{1,0:T(8,128)(2,1)S(1)}, bf16[128,512]{1,0:T(8,128)(2,1)S(1)}, u32[]{:S(2)}, u32[]{:S(2)}) collective-permute-start(bf16[128,512]{1,0:T(8,128)(2,1)S(1)} %attend.5), channel_id=1, source_target_pairs={{0,38},{1,35},{2,32},{3,37},{4,34},{5,39},{6,36},{7,33},{8,46},{9,... | collective-permute-start | bytes 393224 | tf_op jit(solution)/shard_map/ppermute | solution.py:206
  85.8 14.3 %collective-permute-start.12 = (bf16[128,512]{1,0:T(8,128)(2,1)S(1)}, bf16[128,512]{1,0:T(8,128)(2,1)S(1)}, u32[]{:S(2)}, u32[]{:S(2)}) collective-permute-start(bf16[128,512]{1,0:T(8,128)(2,1)S(1)} %attend.6), channel_id=1, source_target_pairs={{0,34},{1,39},{2,36},{3,33},{4,38},{5,35},{6,32},{7,37},{8,42},{9,... | collective-permute-start | bytes 393224 | tf_op jit(solution)/shard_map/ppermute | solution.py:206
  97.5 12.5 %collective-permute-start.14 = (bf16[128,512]{1,0:T(8,128)(2,1)S(1)}, bf16[128,512]{1,0:T(8,128)(2,1)S(1)}, u32[]{:S(2)}, u32[]{:S(2)}) collective-permute-start(bf16[128,512]{1,0:T(8,128)(2,1)S(1)} %attend.7), channel_id=1, source_target_pairs={{0,36},{1,37},{2,38},{3,39},{4,32},{5,33},{6,34},{7,35},{8,44},{9,... | collective-permute-start | bytes 393224 | tf_op jit(solution)/shard_map/ppermute | solution.py:206
